TPU v7x, 32 devices: a whole 2x2x4 slice. The times are simulated.
32 devices in a mesh: leaf: 8 (over y, x, core), rows: 4 (over z).
Axes of the slice: x: 2, y: 2, z: 4, core: 2. Of those that a mesh axis runs over, the one named last changes fastest.
Arguments:
- right_side: float32 [8, 2, 64, 512], P('leaf', None, None, 'rows'), as said below
- diag_inverse: float32 [8, 2, 512, 128], P('leaf', None, 'rows'), as said below
- sep_lower: float32 [8, 2, 512, 512], P('leaf', None, 'rows'), as said below
- front_lower: float32 [8, 2, 1024, 512], P('leaf', None, None, 'rows'), as said below
- front_index: int32 [8, 2, 1024], P('leaf'), may hold values from 0 to 1535, as said below
Outputs:
- solution: float32 [8, 2, 64, 512], P('leaf', None, None, 'rows')
- top_update: float32 [8, 2, 64, 512], P('leaf', None, None, 'rows')
Inputs may be any that keep to these rules, and one draw needn't show every extreme that they name: `front_index`: for each leaf index and slot s the 1024 entries are distinct, lie below (3 - s) * 512, and are the same on all 2**s leaf indices of the slot's subtree. `right_side`: entries of slot s are the same on all 2**s leaf indices of the slot's subtree. `diag_inverse`: entries of slot s are the same on all 2**s leaf indices of the slot's subtree. `sep_lower`: entries of slot s are the same on all 2**s leaf indices of the slot's subtree. `front_lower`: entries of slot s are the same on all 2**s leaf indices of the slot's subtree.
All inputs are finite; a program needn't handle non-finite values.
Results may differ from a plain program's by a relative error of at most 0.00011.
Values sent between devices are 32-bit elements; how exact they have to be, the bound alone decides.
A program may use at most 128 MiB of HBM per device.

v0:
```python
import jax
import jax.numpy as jnp
from jax import lax
from jax.sharding import PartitionSpec as P

exact_precision = lax.Precision.HIGHEST


def partner(value, axis, apart):
    mask = 2**apart
    pairs = [(source, source ^ mask) for source in range(lax.axis_size(axis))]
    return lax.ppermute(value, axis, pairs)


def product(left, right):
    return lax.dot_general(
        left,
        right,
        (((left.ndim - 1,), (right.ndim - 1,)), ((), ())),
        precision=exact_precision,
        preferred_element_type=jnp.float32,
    )


def solve_rows(target, inverse, prefixes, width):
    solved = []
    for block, prefix in enumerate(prefixes):
        first = block * width
        total = target[:, first : first + width]
        if block > 0:
            total = total - product(jnp.concatenate(solved, axis=1), prefix)
        solved.append(product(total, inverse[first : first + width]))
    return jnp.concatenate(solved, axis=1)


def on_device(right_side, diag_inverse, sep_lower, front_lower, front_index):
    levels = right_side.shape[1]
    vectors = right_side.shape[2]
    width = right_side.shape[3]
    blocks = lax.axis_size("rows")
    here = lax.axis_index("rows")
    depth = levels + 1
    targets = right_side[0]
    inverses = diag_inverse[0]
    lowers = sep_lower[0]
    fronts = front_lower[0]
    indices = front_index[0]
    lower_all, inverse_all = (
        lax.all_gather(lowers, "rows", axis=1, tiled=True),
        lax.all_gather(inverses, "rows", axis=1, tiled=True),
    )
    prefix_rows = [
        lower_all[:, block * width : (block + 1) * width, : block * width]
        for block in range(blocks)
    ]
    pending = None
    solutions = []
    for level in range(levels):
        height = depth - level
        if level == 0:
            target = targets[0]
        else:
            pending = pending + partner(pending, "leaf", level - 1)
            target = targets[level] - pending[:, height * width :]
            pending = pending[:, : height * width]
        gathered = lax.all_gather(target, "rows", axis=1, tiled=True)
        joined = solve_rows(
            gathered, inverse_all[level], [rows[level] for rows in prefix_rows], width
        )
        own_block = lax.dynamic_slice_in_dim(joined, here * width, width, 1)
        solutions.append(own_block)
        partial_front = product(own_block, fronts[level])
        summed = lax.psum(partial_front, "rows")
        positions = jnp.arange(height * width, dtype=jnp.int32)
        wanted = positions // width * (blocks * width) + here * width + positions % width
        hits = (wanted[:, None] == indices[level][None, :]).astype(jnp.float32)
        update = product(summed, hits)
        pending = update if level == 0 else pending + update
    top = pending.reshape(vectors, 2, width).transpose(1, 0, 2)
    return (jnp.stack(solutions, axis=0)[None], top[None])


def solution(mesh):
    in_specs = (
        P("leaf", None, None, "rows"),
        P("leaf", None, "rows", None),
        P("leaf", None, "rows", None),
        P("leaf", None, None, "rows"),
        P("leaf", None, None),
    )
    out_specs = (P("leaf", None, None, "rows"), P("leaf", None, None, "rows"))
    return jax.shard_map(
        on_device, mesh=mesh, in_specs=in_specs, out_specs=out_specs, check_vma=False
    )
```

profile of v0, /device:TPU:0, one launch (start us, length us, event | category | flops | bytes accessed | tf_op | source)
XLA Modules:
  0.0 174.2 jit_solution(17245503545314237015)
XLA Ops:
  7.2 0.0 copy-start
  7.2 0.0 copy-start.2
  7.2 0.0 all-gather.5.cloned.1.call-start
  7.2 0.7 all-gather.5.cloned.1.call-update
  7.9 0.0 all-reduce.3.cloned.1.call-start
  8.0 0.8 slice.139
  8.7 0.0 copy-start.1
  8.7 15.2 %all-gather = f32[1,1,64,512]{3,2,1,0:T(8,128)S(1)} all-gather(f32[1,1,64,128]{3,2,1,0:T(8,128)S(1)} %slice.139), channel_id=2, replica_groups=mesh['leaf'=8,'rows'=4] {'rows'}, dimensions={3}, use_global_device_ids=true | all-gather | bytes 163840 | tf_op jit(solution)/shard_map/all_gather | solution.py:66
  24.0 23.7 %all-gather.1 = f32[1,2,512,128]{3,2,1,0:T(8,128)S(1)} all-gather(f32[1,2,128,128]{3,2,1,0:T(8,128)} %param.6), channel_id=3, replica_groups=mesh['leaf'=8,'rows'=4] {'rows'}, dimensions={2}, use_global_device_ids=true | all-gather | bytes 655360 | tf_op jit(solution)/shard_map/all_gather | solution.py:50
  47.7 0.2 fusion.35
  47.9 18.6 %all-gather.5.cloned.1.call-done = f32[1,2,512,512]{3,2,1,0:T(8,128)} async-done(((f32[1,2,128,512]{3,2,1,0:T(8,128)}), f32[1,2,512,512]{3,2,1,0:T(8,128)}) %all-gather.5.cloned.1.call-update) | async-done | bytes 2097168 | tf_op jit(solution)/shard_map/all_gather | solution.py:49
  66.5 1.1 convolution_subtract_fusion.2
  67.6 0.2 fusion.34
  67.9 1.2 convolution_subtract_fusion.1
  69.0 0.2 fusion.33
  69.3 1.3 convolution_subtract_fusion
  70.6 0.2 fusion.32
  70.9 0.0 copy-done
  70.9 1.4 fusion.8
  72.3 0.0 all-reduce.3.cloned.1.call-update
  72.3 0.0 all-reduce.5.cloned.1.call-start
  72.4 0.0 copy-done.2
  72.4 34.6 %all-reduce.3.cloned.1.call-done = f32[64,1024]{1,0:T(8,128)} async-done(((f32[64,1024]{1,0:T(8,128)}), f32[64,1024]{1,0:T(8,128)}) %all-reduce.3.cloned.1.call-update) | async-done | bytes 262160 | tf_op jit(solution)/shard_map/psum | solution.py:73
  107.0 1.9 %fusion = f32[64,384]{1,0:T(8,128)S(1)} fusion(f32[64,1024]{1,0:T(8,128)} %all-reduce.3.cloned.1.call-done, s32[1024]{0:T(1024)S(1)} %bitcast.100, s32[384]{0:T(512)S(1)} %fusion.56), kind=kOutput, calls=%fused_computation | convolution fusion | flops 302383104 | bytes 366080 | tf_op jit(solution)/shard_map/dot_general | solution.py:16
  108.9 0.1 collective-permute-start
  109.0 1.3 collective-permute-done
  110.3 0.0 copy-done.1
  110.3 13.3 %all_gather.15 = f32[64,512]{1,0:T(8,128)S(1)} all-gather(f32[64,128]{1,0:T(8,128)S(1)} %slice_subtract_fusion.6), channel_id=1, replica_groups=mesh['leaf'=8,'rows'=4] {'rows'}, dimensions={1}, use_global_device_ids=true | all-gather | bytes 163840 | tf_op jit(solution)/shard_map/all_gather | solution.py:66
  123.7 0.2 fusion.31
  123.9 1.1 fusion.30
  125.0 0.2 fusion.29
  125.3 1.2 fusion.15
  126.4 0.2 fusion.28
  126.7 1.3 fusion.14
  128.0 0.2 fusion.27
  128.3 1.4 fusion.6
  129.7 0.0 all-reduce.5.cloned.1.call-update
  129.7 0.6 maximum_bitcast_fusion
  130.3 35.0 %all-reduce.5.cloned.1.call-done = f32[64,1024]{1,0:T(8,128)} async-done(((f32[64,1024]{1,0:T(8,128)}), f32[64,1024]{1,0:T(8,128)}) %all-reduce.5.cloned.1.call-update) | async-done | bytes 262160 | tf_op jit(solution)/shard_map/psum | solution.py:73
  165.3 1.6 fusion.26
  167.0 0.6 copy.10
  (7 shorter events, 0.1 us)
Async XLA Ops:
  7.2 63.7 %copy-start = (f32[1,2,1024,128]{3,2,1,0:T(8,128)S(1)}, f32[1,2,1024,128]{3,2,1,0:T(8,128)}, u32[]{:S(2)}) copy-start(f32[1,2,1024,128]{3,2,1,0:T(8,128)} %param.8) | copy-start | bytes 3145732
  7.2 65.2 %copy-start.2 = (s32[1,2,1024]{2,1,0:T(2,128)S(1)}, s32[1,2,1024]{2,1,0:T(2,128)}, u32[]{:S(2)}) copy-start(s32[1,2,1024]{2,1,0:T(2,128)} %param.9) | copy-start | bytes 24580
  7.2 59.4 %all-gather.5.cloned.1.call-start = ((), (), s32[]{:S(2)}) async-start(), calls=%async_computation.2 | async-start | bytes 2621440 | tf_op jit(solution)/shard_map/all_gather | solution.py:49
  7.9 99.1 %all-reduce.3.cloned.1.call-start = ((), (), s32[]{:S(2)}) async-start(), calls=%async_computation | async-start | bytes 524288 | tf_op jit(solution)/shard_map/psum | solution.py:73
  8.7 101.6 %copy-start.1 = (f32[1,2,64,128]{3,2,1,0:T(8,128)S(1)}, f32[1,2,64,128]{3,2,1,0:T(8,128)}, u32[]{:S(2)}) copy-start(f32[1,2,64,128]{3,2,1,0:T(8,128)} %param.5) | copy-start | bytes 196612
  72.3 93.0 %all-reduce.5.cloned.1.call-start = ((), (), s32[]{:S(2)}) async-start(), calls=%async_computation.1 | async-start | bytes 524288 | tf_op jit(solution)/shard_map/psum | solution.py:73
  108.9 1.4 collective-permute-start
Sparse Core Ops, SparseCore 0:
  9.6 56.9 all-gather.4
  72.4 34.5 all-reduce.2
  129.8 35.4 all-reduce.4
where the time goes:
time: 175 us; the launch traced here: 174 us
  waiting for transfers between devices  90.3 us (52%)
  blocking collectives  52.3 us (30%)
  matrix products  15.3 us (9%)
  between operations  13.9 us (8%)
    psum x2, waiting for transfers between devices, on_device(): summed = lax.psum(partial_front, 'rows')  69.7 us
    all_gather x2, blocking collectives, on_device(): gathered = lax.all_gather(target, 'rows', axis=1, tiled=True)  28.6 us
    all_gather x1, blocking collectives, on_device(): lax.all_gather(inverses, 'rows', axis=1, tiled=True)  23.7 us
    all_gather x1, waiting for transfers between devices, on_device(): lax.all_gather(lowers, 'rows', axis=1, tiled=True)  18.6 us
    dot_general x18, matrix products, product(): lax.dot_general(left, right, (((left.ndim - 1,), (right.ndim - 1,)), ((),...  15.3 us
  transfers between devices with their start and end apart: 4, of which 4 were waited for; matrix products, arithmetic and copies ran while one was open for 1% of the time, Pallas kernels for 0%

commit v1 on v0

v1 whole, which is shorter than its diff:
```python
import functools

import jax
import jax.numpy as jnp
from jax import lax
from jax.experimental import pallas as pl
from jax.experimental.pallas import tpu as pltpu
from jax.sharding import PartitionSpec as P

MESH = pl.DeviceIdType.MESH
F32 = jnp.float32
BF16 = jnp.bfloat16


def split(value):
    high = value.astype(BF16)
    low = (value - high.astype(F32)).astype(BF16)
    return high, low


def dot_nt(left, right):
    return lax.dot_general(
        left, right, (((1,), (1,)), ((), ())), preferred_element_type=F32
    )


def product(left, right):
    return (
        dot_nt(left[0], right[1]) + dot_nt(left[1], right[0])
    ) + dot_nt(left[0], right[0])


def kernel(
    blocks,
    rs_ref,
    idx_ref,
    diag_hbm,
    lower_hbm,
    front_hbm,
    sol_ref,
    top_ref,
    ld0,
    ld1,
    front,
    place_t,
    place_u,
    spread,
    gather_f,
    xs,
    part_t,
    part_u,
    recv_t,
    recv_u,
    ag,
    own_half,
    other_half,
    load_sem,
    x_sem,
    ld_sem,
    lf_sem,
    g_sem,
    gf_sem,
    t_sem,
    u_sem,
    ag_sem,
    out_sem,
):
    vectors, width = rs_ref.shape[2], rs_ref.shape[3]
    half = vectors // 2
    sep = blocks * width
    rows_half = width // 2
    leaf = lax.axis_index("leaf")
    me = lax.axis_index("rows")
    core = lax.rem(leaf, 2)
    first_leaf = leaf - core
    partner = (leaf + 1 - 2 * core, me)

    def remote(src, dst, sems, out_slot, in_slot, device):
        return pltpu.make_async_remote_copy(
            src_ref=src,
            dst_ref=dst,
            send_sem=sems.at[0, out_slot],
            recv_sem=sems.at[1, in_slot],
            device_id=device,
            device_id_type=MESH,
        )

    loads = [
        pltpu.make_async_copy(diag_hbm.at[0, 0], ld0.at[:, pl.ds(0, width)], load_sem.at[0]),
        pltpu.make_async_copy(lower_hbm.at[0, 0], ld0.at[:, pl.ds(width, sep)], load_sem.at[1]),
        pltpu.make_async_copy(diag_hbm.at[0, 1], ld1.at[me, :, pl.ds(0, width)], load_sem.at[2]),
        pltpu.make_async_copy(lower_hbm.at[0, 1], ld1.at[me, :, pl.ds(width, sep)], load_sem.at[3]),
        pltpu.make_async_copy(front_hbm.at[0, 0], front.at[0], load_sem.at[4]),
        pltpu.make_async_copy(front_hbm.at[0, 1], front.at[1], load_sem.at[5]),
    ]
    for load in loads:
        load.start()

    barrier = pltpu.get_barrier_semaphore()
    pl.semaphore_signal(barrier, inc=1, device_id=partner, device_id_type=MESH)
    for q in range(blocks):
        @pl.when(q != me)
        def _():
            for c in range(2):
                pl.semaphore_signal(
                    barrier, inc=1, device_id=(first_leaf + c, q), device_id_type=MESH
                )

    def x_copy(q):
        return remote(xs.at[me], xs.at[me], x_sem, q, me, (leaf, q))

    def x_arrival(e):
        return remote(xs.at[e], xs.at[e], x_sem, e, e, (leaf, e))

    def finish_x(total):
        x = product(split(total), split(ld0[:, :width]))
        xs[me] = x
        for q in range(1, blocks):
            @pl.when(q > me)
            def _():
                x_copy(q).start()

    loads[0].wait()
    loads[1].wait()
    pl.semaphore_wait(barrier, 2 * blocks - 1)

    @pl.when(me == 0)
    def _():
        finish_x(rs_ref[0, 0])

    loads[2].wait()
    loads[3].wait()

    def ld_rows(r, c):
        return ld1.at[
            r,
            pl.ds(pl.multiple_of(c * rows_half, rows_half), rows_half),
            pl.ds(0, (r + 1) * width),
        ]

    def ld_own_rows(r):
        return ld1.at[
            me,
            pl.ds(pl.multiple_of(core * rows_half, rows_half), rows_half),
            pl.ds(0, (r + 1) * width),
        ]

    for r in range(blocks):
        @pl.when(me == r)
        def _():
            for q in range(blocks):
                if q != r:
                    remote(ld_rows(r, core), ld_rows(r, core), ld_sem, q, r, (leaf, q)).start()

    lanes = idx_ref.shape[2]

    def hits(first, count, level):
        wanted = first + lax.broadcasted_iota(jnp.int32, (count, lanes), 0)
        return jnp.where(wanted == idx_ref[0, level : level + 1, :], 1.0, 0.0).astype(BF16)

    def placed(marks, both):
        return lax.dot_general(
            marks, both, (((1,), (0,)), ((), ())), preferred_element_type=F32
        )

    loads[4].wait()
    both0 = jnp.concatenate(split(front[0]), axis=1)

    def place_step(q, carry):
        for slot, anc in enumerate((2, 0, 1)):
            rows = placed(hits(anc * sep + q * width, width, 0), both0).astype(BF16)
            for k in range(2):
                piece = rows[:, k * width : (k + 1) * width]
                if slot == 0:
                    place_t[k, q] = piece
                else:
                    place_u[k, q, (slot - 1) * width : slot * width, :] = piece
        return carry

    lax.fori_loop(0, blocks, place_step, 0)
    loads[5].wait()

    def g_copy(q):
        return remote(spread.at[q], gather_f.at[me, core], g_sem, q, me, (leaf, q))

    def g_arrival(r):
        return remote(gather_f.at[r, core], gather_f.at[r, core], g_sem, r, r, (leaf, r))

    def spread_front():
        both1 = jnp.concatenate(split(front[1]), axis=1)

        def step(q, carry):
            rows = placed(hits(core * sep + q * width, width, 1), both1)
            spread[q] = rows[:, :width] + rows[:, width:]
            return carry

        lax.fori_loop(0, blocks, step, 0)
        gather_f[me, core] = spread[me]
        for q in range(blocks):
            @pl.when(q != me)
            def _():
                g_copy(q).start()

    late = blocks // 2

    @pl.when(me >= late)
    def _():
        spread_front()

    @pl.when(me >= 1)
    def _():
        sol_ref[0, 0] = rs_ref[0, 0]
        for e in range(blocks - 1):
            @pl.when(e < me)
            def _():
                right = split(ld0[:, (e + 1) * width : (e + 2) * width])
                x_arrival(e).wait_recv()
                sol_ref[0, 0] = sol_ref[0, 0] - product(split(xs[e]), right)
        finish_x(sol_ref[0, 0])

    x_own = xs[me]
    sol_ref[0, 0] = x_own
    x_parts = split(x_own)

    def piece_copy(parts, lands, sems, q, c):
        return remote(
            parts.at[q, c],
            lands.at[2 * me + core],
            sems,
            2 * q + c,
            2 * me + core,
            (first_leaf + c, q),
        )

    def is_other(q, c):
        return (q != me) | (c != core)

    def send_pieces(parts, lands, sems):
        for q in range(blocks):
            for c in range(2):
                @pl.when(is_other(q, c))
                def _():
                    piece_copy(parts, lands, sems, q, c).start()

    for q in range(blocks):
        update = product(x_parts, (place_t[0, q], place_t[1, q]))
        for c in range(2):
            part_t[q, c] = update[c * half : (c + 1) * half]
    send_pieces(part_t, recv_t, t_sem)
    for q in range(blocks):
        update = product(x_parts, (place_u[0, q], place_u[1, q]))
        for c in range(2):
            part_u[q, c] = update[c * half : (c + 1) * half]

    @pl.when(me < blocks - 1)
    def _():
        send_pieces(part_u, recv_u, u_sem)

    @pl.when(me < late)
    def _():
        spread_front()

    def ld_forward(r):
        return remote(ld_rows(r, core), ld_rows(r, core), lf_sem, r, r, partner)

    def ld_forward_in(r):
        return remote(ld_rows(r, 1 - core), ld_rows(r, 1 - core), lf_sem, r, r, partner)

    def g_forward(r):
        return remote(gather_f.at[r, core], gather_f.at[r, core], gf_sem, r, r, partner)

    def g_forward_in(r):
        return remote(gather_f.at[r, 1 - core], gather_f.at[r, 1 - core], gf_sem, r, r, partner)

    for r in range(blocks):
        @pl.when(r != me)
        def _():
            remote(ld_rows(r, core), ld_rows(r, core), ld_sem, r, r, (leaf, r)).wait_recv()
            ld_forward(r).start()
            g_arrival(r).wait_recv()
        g_forward(r).start()

    def piece_arrival(parts, lands, sems, r, c):
        return remote(parts.at[r, c], lands.at[2 * r + c], sems, 2 * r + c, 2 * r + c, (first_leaf + c, r))

    recv_t[2 * me + core] = part_t[me, core]
    total = None
    for r in range(blocks):
        for c in range(2):
            @pl.when(is_other(r, c))
            def _():
                piece_arrival(part_t, recv_t, t_sem, r, c).wait_recv()
    total = recv_t[0]
    for s in range(1, 2 * blocks):
        total = total + recv_t[s]
    first_row = pl.multiple_of(core * half, half)
    ag[me] = rs_ref[0, 1, pl.ds(first_row, half), :] - total

    def ag_copy(q):
        return remote(ag.at[me], ag.at[me], ag_sem, q, me, (leaf, q))

    for q in range(blocks):
        @pl.when(q != me)
        def _():
            ag_copy(q).start()

    @pl.when(me == blocks - 1)
    def _():
        send_pieces(part_u, recv_u, u_sem)

    for r in range(blocks):
        @pl.when(r != me)
        def _():
            ld_forward_in(r).wait_recv()
        g_forward_in(r).wait_recv()

    solved = []
    top = None
    for b in range(blocks):
        @pl.when(b != me)
        def _():
            remote(ag.at[b], ag.at[b], ag_sem, b, b, (leaf, b)).wait_recv()
        total = ag[b]
        if b > 1:
            older = [jnp.concatenate([x[k] for x in solved[:-1]], axis=1) for k in range(2)]
            total = total - product(older, split(ld1[b, :, width : b * width]))
        if b > 0:
            total = total - product(solved[-1], split(ld1[b, :, b * width : (b + 1) * width]))
        x = product(split(total), split(ld1[b, :, :width]))

        @pl.when(b == me)
        def _():
            own_half[0] = x

        solved.append(split(x))
        added = [
            product(solved[-1], split(gather_f[b, k])) for k in range(2)
        ]
        top = added if top is None else [top[k] + added[k] for k in range(2)]

    def half_copy(k):
        return remote(own_half.at[k], other_half.at[k], out_sem, k, k, partner)

    recv_u[2 * me + core] = part_u[me, core]
    for r in range(blocks):
        for c in range(2):
            @pl.when(is_other(r, c))
            def _():
                piece_arrival(part_u, recv_u, u_sem, r, c).wait_recv()
    slot0 = recv_u[0]
    for s in range(1, 2 * blocks):
        slot0 = slot0 + recv_u[s]
    for k in range(2):
        own_half[1 + k] = top[k] + slot0[:, k * width : (k + 1) * width]
    for k in range(3):
        half_copy(k).start()
    other_row = pl.multiple_of((1 - core) * half, half)
    sol_ref[0, 1, pl.ds(first_row, half), :] = own_half[0]
    for k in range(2):
        top_ref[0, k, pl.ds(first_row, half), :] = own_half[1 + k]

    for q in range(blocks):
        @pl.when(q > me)
        def _():
            x_copy(q).wait_send()
        @pl.when(q != me)
        def _():
            ag_copy(q).wait_send()
            g_copy(q).wait_send()
            ld_forward(q).wait_send()
        g_forward(q).wait_send()
        for c in range(2):
            @pl.when(is_other(q, c))
            def _():
                piece_copy(part_t, recv_t, t_sem, q, c).wait_send()
                piece_copy(part_u, recv_u, u_sem, q, c).wait_send()
    for r in range(blocks):
        @pl.when(me == r)
        def _():
            for q in range(blocks):
                if q != r:
                    remote(ld_rows(r, core), ld_rows(r, core), ld_sem, q, r, (leaf, q)).wait_send()

    for k in range(3):
        half_copy(k).wait()
    sol_ref[0, 1, pl.ds(other_row, half), :] = other_half[0]
    for k in range(2):
        top_ref[0, k, pl.ds(other_row, half), :] = other_half[1 + k]


def on_device(right_side, diag_inverse, sep_lower, front_lower, front_index):
    blocks = lax.axis_size("rows")
    vectors, width = right_side.shape[2:]
    reach = front_lower.shape[2]
    half = vectors // 2
    sep = blocks * width
    vmem = pl.BlockSpec(memory_space=pltpu.VMEM)
    hbm = pl.BlockSpec(memory_space=pl.ANY)
    dma = pltpu.SemaphoreType.DMA
    return pl.pallas_call(
        functools.partial(kernel, blocks),
        out_shape=(
            jax.ShapeDtypeStruct((1, 2, vectors, width), F32),
            jax.ShapeDtypeStruct((1, 2, vectors, width), F32),
        ),
        in_specs=[vmem, vmem, hbm, hbm, hbm],
        out_specs=(vmem, vmem),
        scratch_shapes=[
            pltpu.VMEM((width, sep + width), F32),
            pltpu.VMEM((blocks, width, sep + width), F32),
            pltpu.VMEM((2, reach, width), F32),
            pltpu.VMEM((2, blocks, width, width), BF16),
            pltpu.VMEM((2, blocks, 2 * width, width), BF16),
            pltpu.VMEM((blocks, width, width), F32),
            pltpu.VMEM((blocks, 2, width, width), F32),
            pltpu.VMEM((blocks, vectors, width), F32),
            pltpu.VMEM((blocks, 2, half, width), F32),
            pltpu.VMEM((blocks, 2, half, 2 * width), F32),
            pltpu.VMEM((2 * blocks, half, width), F32),
            pltpu.VMEM((2 * blocks, half, 2 * width), F32),
            pltpu.VMEM((blocks, half, width), F32),
            pltpu.VMEM((3, half, width), F32),
            pltpu.VMEM((3, half, width), F32),
            dma((6,)),
            dma((2, blocks)),
            dma((2, blocks)),
            dma((2, blocks)),
            dma((2, blocks)),
            dma((2, blocks)),
            dma((2, 2 * blocks)),
            dma((2, 2 * blocks)),
            dma((2, blocks)),
            dma((2, 3)),
        ],
        compiler_params=pltpu.CompilerParams(
            collective_id=0, has_side_effects=True, vmem_limit_bytes=60 * 1024 * 1024
        ),
    )(right_side, front_index, diag_inverse, sep_lower, front_lower)


def solution(mesh):
    in_specs = (
        P("leaf", None, None, "rows"),
        P("leaf", None, "rows", None),
        P("leaf", None, "rows", None),
        P("leaf", None, None, "rows"),
        P("leaf", None, None),
    )
    out_specs = (P("leaf", None, None, "rows"), P("leaf", None, None, "rows"))
    return jax.shard_map(
        on_device, mesh=mesh, in_specs=in_specs, out_specs=out_specs, check_vma=False
    )
```

time: 175 us -> 40.4 us (0.23)
  waiting for transfers between devices: 90.3 us -> 0 us
  blocking collectives: 52.3 us -> 0 us
  Pallas kernels: 0 us -> 37.3 us
  matrix products: 15.3 us -> 0 us
  between operations: 13.9 us -> 0.65 us
    psum x2 -> x0, waiting for transfers between devices: 69.7 us -> none  [on_device(): summed = lax.psum(partial_front, 'rows')]
    all_gather x3 -> x0, blocking collectives: 52.3 us -> none  [the longest x2 28.6 us: on_device(): gathered = lax.all_gather(target, 'rows', axis=1, tiled=True)]
    pallas_call x0 -> x1, Pallas kernels: none -> 37.3 us  [on_device(): pl.pallas_call(functools.partial(kernel, blocks), out_shape=(jax.ShapeDty...]
    all_gather x1 -> x0, waiting for transfers between devices: 18.6 us -> none  [on_device(): lax.all_gather(lowers, 'rows', axis=1, tiled=True)]
    dot_general x18 -> x0, matrix products: 15.3 us -> none  [product(): lax.dot_general(left, right, (((left.ndim - 1,), (right.ndim - 1,)), ((),...]
    unnamed x6 -> x4, local copies, waits for them, and re-layouts: 0.01 us -> 2.14 us
  transfers between devices with their start and end apart: 4 -> 0, of which waited for: 4 -> 0; matrix products, arithmetic and copies ran while one was open for 1% -> 0% of each run, Pallas kernels for 0% -> 0%
where the time goes in v1:
time: 40.4 us; the launch traced here: 40.1 us
  Pallas kernels  37.3 us (92%)
  local copies, waits for them, and re-layouts  2.14 us (5%)
  between operations  0.65 us (2%)
    pallas_call x1, Pallas kernels, on_device(): pl.pallas_call(functools.partial(kernel, blocks), out_shape=(jax.ShapeDty...  37.3 us
    unnamed x4, local copies, waits for them, and re-layouts  2.14 us

profile of v1, /device:TPU:0, one launch (start us, length us, event | category | flops | bytes accessed | tf_op | source)
XLA Modules:
  0.0 40.1 jit_solution(15740481215243965808)
XLA Ops:
  0.6 37.3 %shard_map.68 = (f32[1,2,64,128]{3,2,1,0:T(8,128)}, f32[1,2,64,128]{3,2,1,0:T(8,128)}) custom-call(f32[1,2,64,128]{3,2,1,0:T(8,128)} %rs_ref.1, s32[1,2,1024]{2,1,0:T(2,128)} %idx_ref.1, f32[1,2,128,128]{3,2,1,0:T(8,128)} %diag_hbm.1, f32[1,2,128,512]{3,2,1,0:T(8,128)} %lower_hbm.1, f32[1,2,1024,128]{3,2,1,0:T(8,128)} %front_hbm.1), custom_call_target="tpu_custom_call" | custom-call | tf_op jit(solution)/shard_map/pallas_call | solution.py:400
  38.0 0.0 copy-start
  38.0 1.5 %copy.9 = f32[1,2,64,128]{3,2,1,0:T(8,128)} copy(f32[1,2,64,128]{3,2,1,0:T(8,128)} %get-tuple-element.4) | data formatting | bytes 131072
  39.5 0.0 copy-done
  39.5 0.6 %copy.10 = f32[1,2,64,128]{3,2,1,0:T(8,128)} copy(f32[1,2,64,128]{3,2,1,0:T(8,128)S(1)} %copy-done) | data formatting | bytes 131072
Async XLA Ops:
  38.0 1.5 %copy-start = (f32[1,2,64,128]{3,2,1,0:T(8,128)S(1)}, f32[1,2,64,128]{3,2,1,0:T(8,128)}, u32[]{:S(2)}) copy-start(f32[1,2,64,128]{3,2,1,0:T(8,128)} %get-tuple-element.5) | copy-start | bytes 196612

commit v2 on v0

v2 whole, which is shorter than its diff:
```python
import functools

import jax
import jax.numpy as jnp
from jax import lax
from jax.experimental import pallas as pl
from jax.experimental.pallas import tpu as pltpu
from jax.sharding import PartitionSpec as P

MESH = pl.DeviceIdType.MESH
F32 = jnp.float32
BF16 = jnp.bfloat16


def split(value):
    high = value.astype(BF16)
    low = (value - high.astype(F32)).astype(BF16)
    return high, low


def dot_nt(left, right):
    return lax.dot_general(
        left, right, (((1,), (1,)), ((), ())), preferred_element_type=F32
    )


def product(left, right):
    return (
        dot_nt(left[0], right[1]) + dot_nt(left[1], right[0])
    ) + dot_nt(left[0], right[0])


def kernel(
    blocks,
    rs_ref,
    idx_ref,
    diag_hbm,
    lower_hbm,
    front_hbm,
    sol_ref,
    top_ref,
    factor,
    front,
    weight,
    place_t,
    place_u,
    place_v,
    total,
    xs0,
    xs1,
    part_t,
    recv_t,
    part_u,
    recv_u,
    part_v,
    recv_v,
    top_half,
    top_other,
    x_other,
    load_sem,
    x0_sem,
    x1_sem,
    t_sem,
    v_sem,
    pair_sem,
):
    vectors, width = rs_ref.shape[2], rs_ref.shape[3]
    half = vectors // 2
    sep = blocks * width
    lanes = idx_ref.shape[2]
    leaf = lax.axis_index("leaf")
    me = lax.axis_index("rows")
    core = lax.rem(leaf, 2)
    first_leaf = leaf - core
    partner = (leaf + 1 - 2 * core, me)
    first_row = pl.multiple_of(core * half, half)
    other_row = pl.multiple_of((1 - core) * half, half)

    def remote(src, dst, sems, out_slot, in_slot, device):
        return pltpu.make_async_remote_copy(
            src_ref=src,
            dst_ref=dst,
            send_sem=sems.at[0, out_slot],
            recv_sem=sems.at[1, in_slot],
            device_id=device,
            device_id_type=MESH,
        )

    barrier = pltpu.get_barrier_semaphore()
    pl.semaphore_signal(barrier, inc=1, device_id=partner, device_id_type=MESH)
    for q in range(blocks):
        @pl.when(q != me)
        def _():
            for c in range(2):
                pl.semaphore_signal(
                    barrier, inc=1, device_id=(first_leaf + c, q), device_id_type=MESH
                )

    loads = []
    for level in range(2):
        for src, dst in (
            (diag_hbm.at[0, level], factor.at[level, :, pl.ds(0, width)]),
            (lower_hbm.at[0, level], factor.at[level, :, pl.ds(width, sep)]),
            (front_hbm.at[0, level], front.at[level]),
        ):
            loads.append(pltpu.make_async_copy(src, dst, load_sem.at[len(loads)]))
    for load in loads:
        load.start()

    def split_factor(level):
        loads[3 * level].wait()
        loads[3 * level + 1].wait()
        for k, piece in enumerate(split(factor[level])):
            weight[level, k] = piece

    def weights(level, b):
        return tuple(weight[level, k, :, b * width : (b + 1) * width] for k in range(2))

    split_factor(0)

    @pl.when(me == 0)
    def _():
        xs0[me] = product(split(rs_ref[0, 0]), weights(0, 0))

    def hits(first, level):
        wanted = first + lax.broadcasted_iota(jnp.int32, (width, lanes), 0)
        return jnp.where(wanted == idx_ref[0, level : level + 1, :], 1.0, 0.0).astype(BF16)

    def placed(marks, both):
        return lax.dot_general(
            marks, both, (((1,), (0,)), ((), ())), preferred_element_type=F32
        ).astype(BF16)

    loads[2].wait()
    both0 = jnp.concatenate(split(front[0]), axis=1)

    def place_step0(q, carry):
        for slot, anc in enumerate((2, 0, 1)):
            rows = placed(hits(anc * sep + q * width, 0), both0)
            for k in range(2):
                piece = rows[:, k * width : (k + 1) * width]
                if slot == 0:
                    place_t[k, q] = piece
                else:
                    place_u[k, q, (slot - 1) * width : slot * width, :] = piece
        return carry

    lax.fori_loop(0, blocks, place_step0, 0)
    split_factor(1)
    loads[5].wait()
    both1 = jnp.concatenate(split(front[1]), axis=1)

    def place_step1(q, carry):
        for slot in range(2):
            rows = placed(hits(slot * sep + q * width, 1), both1)
            for k in range(2):
                piece = rows[:, k * width : (k + 1) * width]
                place_v[k, q, slot * width : (slot + 1) * width, :] = piece
        return carry

    lax.fori_loop(0, blocks, place_step1, 0)

    pl.semaphore_wait(barrier, 2 * blocks - 1)

    def x_copy(xs, sems, q):
        return remote(xs.at[me], xs.at[me], sems, q, me, (leaf, q))

    def send_x(xs, sems):
        for q in range(1, blocks):
            @pl.when(q > me)
            def _():
                x_copy(xs, sems, q).start()

    def subtract_solved(level, xs, sems, rows):
        for e in range(blocks - 1):
            @pl.when(e < me)
            def _():
                right = weights(level, e + 1)
                remote(xs.at[e], xs.at[e], sems, e, e, (leaf, e)).wait_recv()
                total[:rows] = total[:rows] - product(split(xs[e]), right)

    @pl.when(me >= 1)
    def _():
        total[...] = rs_ref[0, 0]
        subtract_solved(0, xs0, x0_sem, vectors)
        xs0[me] = product(split(total[...]), weights(0, 0))

    send_x(xs0, x0_sem)
    x_parts = split(xs0[me])

    def is_other(q, c):
        return (q != me) | (c != core)

    def t_copy(q, c):
        return remote(
            part_t.at[q, c],
            recv_t.at[2 * me + core],
            t_sem,
            2 * q + c,
            2 * me + core,
            (first_leaf + c, q),
        )

    for q in range(blocks):
        update = product(x_parts, (place_t[0, q], place_t[1, q]))
        for c in range(2):
            part_t[q, c] = update[c * half : (c + 1) * half]
        for c in range(2):
            @pl.when(is_other(q, c))
            def _():
                t_copy(q, c).start()
    sol_ref[0, 0] = xs0[me]
    for q in range(blocks):
        update = product(x_parts, (place_u[0, q], place_u[1, q]))
        for c in range(2):
            part_u[c, q] = update[c * half : (c + 1) * half]

    u_copy = remote(part_u.at[1 - core], recv_u, pair_sem, 0, 0, partner)
    u_copy.start()
    total[:half] = rs_ref[0, 1, pl.ds(first_row, half), :] - part_t[me, core]
    u_copy.wait_recv()
    for q in range(blocks):
        part_v[q] = part_u[core, q] + recv_u[q]
    for r in range(blocks):
        for c in range(2):
            @pl.when(is_other(r, c))
            def _():
                s = 2 * r + c
                remote(part_t.at[r, c], recv_t.at[s], t_sem, s, s, (first_leaf + c, r)).wait_recv()
                total[:half] = total[:half] - recv_t[s]

    subtract_solved(1, xs1, x1_sem, half)
    xs1[me] = product(split(total[:half]), weights(1, 0))
    send_x(xs1, x1_sem)
    x_out = remote(xs1.at[me], x_other, pair_sem, 1, 1, partner)
    x_parts = split(xs1[me])

    def v_copy(q):
        return remote(part_v.at[q], recv_v.at[me], v_sem, q, me, (leaf, q))

    for q in range(blocks):
        part_v[q] = part_v[q] + product(x_parts, (place_v[0, q], place_v[1, q]))

        @pl.when(q != me)
        def _():
            v_copy(q).start()

    x_out.start()
    sol_ref[0, 1, pl.ds(first_row, half), :] = xs1[me]
    top_half[...] = part_v[me]
    for r in range(blocks):
        @pl.when(r != me)
        def _():
            remote(part_v.at[r], recv_v.at[r], v_sem, r, r, (leaf, r)).wait_recv()
            top_half[...] = top_half[...] + recv_v[r]
    top_out = remote(top_half, top_other, pair_sem, 2, 2, partner)
    top_out.start()
    for k in range(2):
        top_ref[0, k, pl.ds(first_row, half), :] = top_half[:, k * width : (k + 1) * width]
    u_copy.wait_send()
    for q in range(blocks):
        @pl.when(q > me)
        def _():
            x_copy(xs0, x0_sem, q).wait_send()
            x_copy(xs1, x1_sem, q).wait_send()
        @pl.when(q != me)
        def _():
            v_copy(q).wait_send()
        for c in range(2):
            @pl.when(is_other(q, c))
            def _():
                t_copy(q, c).wait_send()
    x_out.wait()
    sol_ref[0, 1, pl.ds(other_row, half), :] = x_other[...]
    top_out.wait()
    for k in range(2):
        top_ref[0, k, pl.ds(other_row, half), :] = top_other[:, k * width : (k + 1) * width]


def on_device(right_side, diag_inverse, sep_lower, front_lower, front_index):
    blocks = lax.axis_size("rows")
    vectors, width = right_side.shape[2:]
    reach = front_lower.shape[2]
    half = vectors // 2
    sep = blocks * width
    vmem = pl.BlockSpec(memory_space=pltpu.VMEM)
    hbm = pl.BlockSpec(memory_space=pl.ANY)
    dma = pltpu.SemaphoreType.DMA
    return pl.pallas_call(
        functools.partial(kernel, blocks),
        out_shape=(
            pltpu.VMEM((1, 2, vectors, width), F32),
            pltpu.VMEM((1, 2, vectors, width), F32),
        ),
        in_specs=[vmem, vmem, hbm, hbm, hbm],
        out_specs=(vmem, vmem),
        scratch_shapes=[
            pltpu.VMEM((2, width, sep + width), F32),
            pltpu.VMEM((2, reach, width), F32),
            pltpu.VMEM((2, 2, width, sep + width), BF16),
            pltpu.VMEM((2, blocks, width, width), BF16),
            pltpu.VMEM((2, blocks, 2 * width, width), BF16),
            pltpu.VMEM((2, blocks, 2 * width, width), BF16),
            pltpu.VMEM((vectors, width), F32),
            pltpu.VMEM((blocks, vectors, width), F32),
            pltpu.VMEM((blocks, half, width), F32),
            pltpu.VMEM((blocks, 2, half, width), F32),
            pltpu.VMEM((2 * blocks, half, width), F32),
            pltpu.VMEM((2, blocks, half, 2 * width), F32),
            pltpu.VMEM((blocks, half, 2 * width), F32),
            pltpu.VMEM((blocks, half, 2 * width), F32),
            pltpu.VMEM((blocks, half, 2 * width), F32),
            pltpu.VMEM((half, 2 * width), F32),
            pltpu.VMEM((half, 2 * width), F32),
            pltpu.VMEM((half, width), F32),
            dma((6,)),
            dma((2, blocks)),
            dma((2, blocks)),
            dma((2, 2 * blocks)),
            dma((2, blocks)),
            dma((2, 3)),
        ],
        compiler_params=pltpu.CompilerParams(
            collective_id=0, has_side_effects=True, vmem_limit_bytes=60 * 1024 * 1024
        ),
    )(right_side, front_index, diag_inverse, sep_lower, front_lower)


def solution(mesh):
    in_specs = (
        P("leaf", None, None, "rows"),
        P("leaf", None, "rows", None),
        P("leaf", None, "rows", None),
        P("leaf", None, None, "rows"),
        P("leaf", None, None),
    )
    out_specs = (P("leaf", None, None, "rows"), P("leaf", None, None, "rows"))
    return jax.shard_map(
        on_device, mesh=mesh, in_specs=in_specs, out_specs=out_specs, check_vma=False
    )
```

time: 175 us -> 38.1 us (0.22)
  waiting for transfers between devices: 90.3 us -> 0 us
  blocking collectives: 52.3 us -> 0 us
  Pallas kernels: 0 us -> 36 us
  matrix products: 15.3 us -> 0 us
  between operations: 13.9 us -> 0.64 us
    psum x2 -> x0, waiting for transfers between devices: 69.7 us -> none  [on_device(): summed = lax.psum(partial_front, 'rows')]
    all_gather x3 -> x0, blocking collectives: 52.3 us -> none  [the longest x2 28.6 us: on_device(): gathered = lax.all_gather(target, 'rows', axis=1, tiled=True)]
    pallas_call x0 -> x1, Pallas kernels: none -> 36 us  [on_device(): pl.pallas_call(functools.partial(kernel, blocks), out_shape=(pltpu.VMEM((...]
    all_gather x1 -> x0, waiting for transfers between devices: 18.6 us -> none  [on_device(): lax.all_gather(lowers, 'rows', axis=1, tiled=True)]
    dot_general x18 -> x0, matrix products: 15.3 us -> none  [product(): lax.dot_general(left, right, (((left.ndim - 1,), (right.ndim - 1,)), ((),...]
  transfers between devices with their start and end apart: 4 -> 0, of which waited for: 4 -> 0; matrix products, arithmetic and copies ran while one was open for 1% -> 0% of each run, Pallas kernels for 0% -> 0%
where the time goes in v2:
time: 38.1 us; the launch traced here: 37.9 us
  Pallas kernels  36 us (94%)
  local copies, waits for them, and re-layouts  1.26 us (3%)
  between operations  0.64 us (2%)
    pallas_call x1, Pallas kernels, on_device(): pl.pallas_call(functools.partial(kernel, blocks), out_shape=(pltpu.VMEM((...  36 us
    unnamed x2, local copies, waits for them, and re-layouts  1.26 us

profile of v2, /device:TPU:0, one launch (start us, length us, event | category | flops | bytes accessed | tf_op | source)
XLA Modules:
  0.0 37.9 jit_solution(17355266430044013701)
XLA Ops:
  0.6 36.0 %shard_map.68 = (f32[1,2,64,128]{3,2,1,0:T(8,128)S(1)}, f32[1,2,64,128]{3,2,1,0:T(8,128)S(1)}) custom-call(f32[1,2,64,128]{3,2,1,0:T(8,128)} %rs_ref.1, s32[1,2,1024]{2,1,0:T(2,128)} %idx_ref.1, f32[1,2,128,128]{3,2,1,0:T(8,128)} %diag_hbm.1, f32[1,2,128,512]{3,2,1,0:T(8,128)} %lower_hbm.1, f32[1,2,1024,128]{3,2,1,0:T(8,128)} %front_hbm.1), custom_call_target="tpu_custom_call" | custom-call | tf_op jit(solution)/shard_map/pallas_call | solution.py:289
  36.6 0.6 %copy.9 = f32[1,2,64,128]{3,2,1,0:T(8,128)} copy(f32[1,2,64,128]{3,2,1,0:T(8,128)S(1)} %get-tuple-element.2) | data formatting | bytes 131072
  37.3 0.6 %copy.10 = f32[1,2,64,128]{3,2,1,0:T(8,128)} copy(f32[1,2,64,128]{3,2,1,0:T(8,128)S(1)} %get-tuple-element.3) | data formatting | bytes 131072

commit v3 on v2

--- a/solution.py
+++ b/solution.py
@@ -40,6 +40,7 @@
     sol_ref,
     top_ref,
     factor,
+    rows1,
     front,
     weight,
     place_t,
@@ -58,6 +59,8 @@
     top_other,
     x_other,
     load_sem,
+    ld_sem,
+    lf_sem,
     x0_sem,
     x1_sem,
     t_sem,
@@ -96,31 +99,31 @@
                     barrier, inc=1, device_id=(first_leaf + c, q), device_id_type=MESH
                 )
 
+    center = blocks // 2
+    groups = min(blocks, 4)
+    per = blocks // groups
     loads = []
-    for level in range(2):
+    for level, held in enumerate((factor, rows1.at[me])):
         for src, dst in (
-            (diag_hbm.at[0, level], factor.at[level, :, pl.ds(0, width)]),
-            (lower_hbm.at[0, level], factor.at[level, :, pl.ds(width, sep)]),
+            (diag_hbm.at[0, level], held.at[:, pl.ds(0, width)]),
+            (lower_hbm.at[0, level], held.at[:, pl.ds(width, sep)]),
             (front_hbm.at[0, level], front.at[level]),
         ):
             loads.append(pltpu.make_async_copy(src, dst, load_sem.at[len(loads)]))
     for load in loads:
         load.start()
 
-    def split_factor(level):
-        loads[3 * level].wait()
-        loads[3 * level + 1].wait()
-        for k, piece in enumerate(split(factor[level])):
-            weight[level, k] = piece
-
-    def weights(level, b):
-        return tuple(weight[level, k, :, b * width : (b + 1) * width] for k in range(2))
-
-    split_factor(0)
+    loads[0].wait()
+    loads[1].wait()
+    for k, piece in enumerate(split(factor[...])):
+        weight[k] = piece
+
+    def weights(b):
+        return tuple(weight[k, :, b * width : (b + 1) * width] for k in range(2))
 
     @pl.when(me == 0)
     def _():
-        xs0[me] = product(split(rs_ref[0, 0]), weights(0, 0))
+        xs0[me] = product(split(rs_ref[0, 0]), weights(0))
 
     def hits(first, level):
         wanted = first + lax.broadcasted_iota(jnp.int32, (width, lanes), 0)
@@ -146,7 +149,8 @@
         return carry
 
     lax.fori_loop(0, blocks, place_step0, 0)
-    split_factor(1)
+    loads[3].wait()
+    loads[4].wait()
     loads[5].wait()
     both1 = jnp.concatenate(split(front[1]), axis=1)
 
@@ -162,53 +166,91 @@
 
     pl.semaphore_wait(barrier, 2 * blocks - 1)
 
-    def x_copy(xs, sems, q):
-        return remote(xs.at[me], xs.at[me], sems, q, me, (leaf, q))
-
-    def send_x(xs, sems):
+    def x_copy(q):
+        return remote(xs0.at[me], xs0.at[me], x0_sem, q, me, (leaf, q))
+
+    def send_x():
         for q in range(1, blocks):
             @pl.when(q > me)
             def _():
-                x_copy(xs, sems, q).start()
-
-    def subtract_solved(level, xs, sems, rows):
+                x_copy(q).start()
+
+    def half_rows(r, c):
+        return rows1.at[
+            r,
+            pl.ds(pl.multiple_of(c * (width // 2), width // 2), width // 2),
+            pl.ds(0, (r + 1) * width),
+        ]
+
+    def row_copy(r):
+        part = half_rows(r, core)
+        return remote(part, part, ld_sem, r, r, (leaf, center))
+
+    def row_forward(r, c):
+        part = half_rows(r, c)
+        return remote(part, part, lf_sem, r, r, partner)
+
+    outer = [r for r in range(blocks) if r != center]
+
+    @pl.when(me == 0)
+    def _():
+        send_x()
+
+    for r in outer:
+        @pl.when(me == r)
+        def _():
+            row_copy(r).start()
+
+    @pl.when(me >= 1)
+    def _():
+        total[...] = rs_ref[0, 0]
         for e in range(blocks - 1):
             @pl.when(e < me)
             def _():
-                right = weights(level, e + 1)
-                remote(xs.at[e], xs.at[e], sems, e, e, (leaf, e)).wait_recv()
-                total[:rows] = total[:rows] - product(split(xs[e]), right)
-
-    @pl.when(me >= 1)
-    def _():
-        total[...] = rs_ref[0, 0]
-        subtract_solved(0, xs0, x0_sem, vectors)
-        xs0[me] = product(split(total[...]), weights(0, 0))
-
-    send_x(xs0, x0_sem)
+                right = weights(e + 1)
+                remote(xs0.at[e], xs0.at[e], x0_sem, e, e, (leaf, e)).wait_recv()
+                total[...] = total[...] - product(split(xs0[e]), right)
+        xs0[me] = product(split(total[...]), weights(0))
+        send_x()
+
     x_parts = split(xs0[me])
 
-    def is_other(q, c):
-        return (q != me) | (c != core)
-
-    def t_copy(q, c):
+    def is_other(r, c):
+        return (r != me) | (c != core)
+
+    def t_copy(g, c):
+        span = pl.ds(g * per, per)
         return remote(
-            part_t.at[q, c],
-            recv_t.at[2 * me + core],
+            part_t.at[c, span],
+            recv_t.at[2 * me + core, span],
             t_sem,
-            2 * q + c,
-            2 * me + core,
-            (first_leaf + c, q),
+            groups * c + g,
+            groups * (2 * me + core) + g,
+            (first_leaf + c, center),
         )
 
+    def t_arrival(r, c, g):
+        span = pl.ds(g * per, per)
+        s = 2 * r + c
+        return pltpu.make_async_remote_copy(
+            src_ref=part_t.at[c, span],
+            dst_ref=recv_t.at[s, span],
+            send_sem=t_sem.at[0, g],
+            recv_sem=t_sem.at[1, groups * s + g],
+            device_id=(first_leaf + c, r),
+            device_id_type=MESH,
+        )
+
     for q in range(blocks):
         update = product(x_parts, (place_t[0, q], place_t[1, q]))
+        update = update - jnp.where((me == q) & (core == 0), rs_ref[0, 1], 0.0)
         for c in range(2):
-            part_t[q, c] = update[c * half : (c + 1) * half]
-        for c in range(2):
-            @pl.when(is_other(q, c))
-            def _():
-                t_copy(q, c).start()
+            part_t[c, q] = update[c * half : (c + 1) * half]
+        if (q + 1) % per == 0:
+            for c in range(2):
+                @pl.when((me != center) | (c != core))
+                def _():
+                    t_copy(q // per, c).start()
     sol_ref[0, 0] = xs0[me]
     for q in range(blocks):
         update = product(x_parts, (place_u[0, q], place_u[1, q]))
@@ -217,21 +259,53 @@
 
     u_copy = remote(part_u.at[1 - core], recv_u, pair_sem, 0, 0, partner)
     u_copy.start()
-    total[:half] = rs_ref[0, 1, pl.ds(first_row, half), :] - part_t[me, core]
     u_copy.wait_recv()
     for q in range(blocks):
         part_v[q] = part_u[core, q] + recv_u[q]
-    for r in range(blocks):
-        for c in range(2):
-            @pl.when(is_other(r, c))
-            def _():
-                s = 2 * r + c
-                remote(part_t.at[r, c], recv_t.at[s], t_sem, s, s, (first_leaf + c, r)).wait_recv()
-                total[:half] = total[:half] - recv_t[s]
-
-    subtract_solved(1, xs1, x1_sem, half)
-    xs1[me] = product(split(total[:half]), weights(1, 0))
-    send_x(xs1, x1_sem)
+
+    def x1_copy(b):
+        return remote(xs1.at[b], xs1.at[b], x1_sem, b, b, (leaf, b))
+
+    @pl.when(me == center)
+    def _():
+        for r in outer:
+            row_copy(r).wait_recv()
+            row_forward(r, core).start()
+        recv_t[2 * center + core] = part_t[core]
+        for r in outer:
+            row_forward(r, 1 - core).wait_recv()
+        solved = []
+        for b in range(blocks):
+            if b % per == 0:
+                for r in range(blocks):
+                    for c in range(2):
+                        @pl.when(is_other(r, c))
+                        def _():
+                            t_arrival(r, c, b // per).wait_recv()
+            value = -recv_t[0, b]
+            for s in range(1, 2 * blocks):
+                value = value - recv_t[s, b]
+            if b > 1:
+                older = [jnp.concatenate([x[k] for x in solved[:-1]], axis=1) for k in range(2)]
+                value = value - product(older, split(rows1[b, :, width : b * width]))
+            if b > 0:
+                value = value - product(
+                    solved[-1], split(rows1[b, :, b * width : (b + 1) * width])
+                )
+            x = product(split(value), split(rows1[b, :, :width]))
+            xs1[b] = x
+            if b != center:
+                x1_copy(b).start()
+            solved.append(split(x))
+        for r in outer:
+            row_forward(r, core).wait_send()
+            x1_copy(r).wait_send()
+
+    for r in outer:
+        @pl.when(me == r)
+        def _():
+            x1_copy(r).wait_recv()
+
     x_out = remote(xs1.at[me], x_other, pair_sem, 1, 1, partner)
     x_parts = split(xs1[me])
 
@@ -258,18 +332,22 @@
     for k in range(2):
         top_ref[0, k, pl.ds(first_row, half), :] = top_half[:, k * width : (k + 1) * width]
     u_copy.wait_send()
+    for c in range(2):
+        @pl.when((me != center) | (c != core))
+        def _():
+            for g in range(groups):
+                t_copy(g, c).wait_send()
+    for r in outer:
+        @pl.when(me == r)
+        def _():
+            row_copy(r).wait_send()
     for q in range(blocks):
         @pl.when(q > me)
         def _():
-            x_copy(xs0, x0_sem, q).wait_send()
-            x_copy(xs1, x1_sem, q).wait_send()
+            x_copy(q).wait_send()
         @pl.when(q != me)
         def _():
             v_copy(q).wait_send()
-        for c in range(2):
-            @pl.when(is_other(q, c))
-            def _():
-                t_copy(q, c).wait_send()
     x_out.wait()
     sol_ref[0, 1, pl.ds(other_row, half), :] = x_other[...]
     top_out.wait()
@@ -295,17 +373,18 @@
         in_specs=[vmem, vmem, hbm, hbm, hbm],
         out_specs=(vmem, vmem),
         scratch_shapes=[
-            pltpu.VMEM((2, width, sep + width), F32),
+            pltpu.VMEM((width, sep + width), F32),
+            pltpu.VMEM((blocks, width, sep + width), F32),
             pltpu.VMEM((2, reach, width), F32),
-            pltpu.VMEM((2, 2, width, sep + width), BF16),
+            pltpu.VMEM((2, width, sep + width), BF16),
             pltpu.VMEM((2, blocks, width, width), BF16),
             pltpu.VMEM((2, blocks, 2 * width, width), BF16),
             pltpu.VMEM((2, blocks, 2 * width, width), BF16),
             pltpu.VMEM((vectors, width), F32),
             pltpu.VMEM((blocks, vectors, width), F32),
             pltpu.VMEM((blocks, half, width), F32),
-            pltpu.VMEM((blocks, 2, half, width), F32),
-            pltpu.VMEM((2 * blocks, half, width), F32),
+            pltpu.VMEM((2, blocks, half, width), F32),
+            pltpu.VMEM((2 * blocks, blocks, half, width), F32),
             pltpu.VMEM((2, blocks, half, 2 * width), F32),
             pltpu.VMEM((blocks, half, 2 * width), F32),
             pltpu.VMEM((blocks, half, 2 * width), F32),
@@ -316,7 +395,9 @@
             dma((6,)),
             dma((2, blocks)),
             dma((2, blocks)),
-            dma((2, 2 * blocks)),
+            dma((2, blocks)),
+            dma((2, blocks)),
+            dma((2, 2 * blocks * min(blocks, 4))),
             dma((2, blocks)),
             dma((2, 3)),
         ],

time: 38.1 us -> 35 us (0.919)
  Pallas kernels: 36 us -> 33 us
    pallas_call x1, Pallas kernels: 36 us -> 33 us  [on_device(): pl.pallas_call(functools.partial(kernel, blocks), out_shape=(pltpu.VMEM((...]
where the time goes in v3:
time: 35 us; the launch traced here: 34.9 us
  Pallas kernels  33 us (94%)
  local copies, waits for them, and re-layouts  1.26 us (4%)
  between operations  0.64 us (2%)
    pallas_call x1, Pallas kernels, on_device(): pl.pallas_call(functools.partial(kernel, blocks), out_shape=(pltpu.VMEM((...  33 us
    unnamed x2, local copies, waits for them, and re-layouts  1.26 us

profile of v3, /device:TPU:0, one launch (start us, length us, event | category | flops | bytes accessed | tf_op | source)
XLA Modules:
  0.0 34.9 jit_solution(18195916311365472051)
XLA Ops:
  0.6 33.0 %shard_map.68 = (f32[1,2,64,128]{3,2,1,0:T(8,128)S(1)}, f32[1,2,64,128]{3,2,1,0:T(8,128)S(1)}) custom-call(f32[1,2,64,128]{3,2,1,0:T(8,128)} %rs_ref.1, s32[1,2,1024]{2,1,0:T(2,128)} %idx_ref.1, f32[1,2,128,128]{3,2,1,0:T(8,128)} %diag_hbm.1, f32[1,2,128,512]{3,2,1,0:T(8,128)} %lower_hbm.1, f32[1,2,1024,128]{3,2,1,0:T(8,128)} %front_hbm.1), custom_call_target="tpu_custom_call" | custom-call | tf_op jit(solution)/shard_map/pallas_call | solution.py:367
  33.6 0.6 %copy.9 = f32[1,2,64,128]{3,2,1,0:T(8,128)} copy(f32[1,2,64,128]{3,2,1,0:T(8,128)S(1)} %get-tuple-element.2) | data formatting | bytes 131072
  34.2 0.6 %copy.10 = f32[1,2,64,128]{3,2,1,0:T(8,128)} copy(f32[1,2,64,128]{3,2,1,0:T(8,128)S(1)} %get-tuple-element.3) | data formatting | bytes 131072
